TPU v7x, 32 devices: a whole 2x2x4 slice. The times are simulated.
32 devices in a mesh: rows: 8 (over z, x), cols: 4 (over y, core).
Axes of the slice: x: 2, y: 2, z: 4, core: 2. Of those that a mesh axis runs over, the one named last changes fastest.
Arguments:
- densities: bfloat16 [6, 2048, 128, 128], P(None, ('rows', 'cols')), may hold values from -6 to 6
- residuals: bfloat16 [6, 2048, 128, 128], P(None, ('rows', 'cols')), may hold values from -32 to 32
- block_pairs: int32 [2, 2048], P(None, ('rows', 'cols')), may hold values from 0 to 1562
- new_owner: int32 [2048], P(('rows', 'cols')), may hold values from -1 to 7, as said below
Outputs:
- owned_blocks: bfloat16 [1024, 128, 128], P(('rows', 'cols'))
- coefficients: float32 [6], replicated
Inputs may be any that keep to these rules, and one draw needn't show every extreme that they name: A live block stays at its index of cols and moves to index new_owner of rows. For each index of cols, every index of rows becomes the owner of exactly 32 blocks, and at most 8 of them come from one device.
All inputs are finite; a program needn't handle non-finite values.
Results may differ from a plain program's by a relative error of at most 0.0019.
Values may be sent and summed in bfloat16 or wider, within the bound.
No kernel may reach another device: no remote copies, remote signals or barrier semaphores. Data moves between devices by JAX's collectives and lax.ppermute only.
A program may use at most 128 MiB of HBM per device.

v0:
```python
import jax
import jax.numpy as jnp
from jax import lax
from jax.sharding import PartitionSpec as P

OWNED = 32


mix_weight = 0.3


def small_solve(system, vector):
    order_n = system.shape[0]
    positions = jnp.arange(order_n, dtype=jnp.int32)
    for step_index in range(order_n):
        column = system[:, step_index] / system[step_index, step_index]
        column = jnp.where(positions > step_index, column, 0.0)
        system = system - column[:, None] * system[step_index][None, :]
        vector = vector - column * vector[step_index]
    solution = jnp.zeros((order_n,), jnp.float32)
    for step_index in reversed(range(order_n)):
        inner = jnp.sum(jnp.where(positions > step_index, system[step_index] * solution, 0.0))
        solution = solution.at[step_index].set(
            (vector[step_index] - inner) / system[step_index, step_index]
        )
    return solution


def slot_correlation(residual_set, weights):
    flattened = residual_set.reshape(residual_set.shape[0], residual_set.shape[1], -1)
    per_slot = jnp.einsum("isn,ksn->sik", flattened, flattened, preferred_element_type=jnp.float32)
    return jnp.einsum("s,sik->ik", weights, per_slot)


def blend_history(density_set, residual_set, coefficients):
    running = jnp.zeros(density_set.shape[1:], jnp.float32)
    for hist_index in range(density_set.shape[0]):
        running = running + coefficients[hist_index] * (
            density_set[hist_index].astype(jnp.float32)
            + mix_weight * residual_set[hist_index].astype(jnp.float32)
        )
    return running.astype(jnp.bfloat16)


def compact_order(arrived_weights):
    usable = arrived_weights > 0.0
    position = jnp.cumsum(usable.astype(jnp.int32)) - 1
    spots = jnp.where(usable, position, OWNED)
    count_in = arrived_weights.shape[0]
    return (
        jnp.zeros((OWNED,), jnp.int32)
        .at[spots]
        .set(jnp.arange(count_in, dtype=jnp.int32), mode="drop")
    )


def on_device(densities, residuals, block_pairs, new_owner):
    rows_count = lax.axis_size("rows")
    held_slots = new_owner.shape[0]
    pair_cap = 2 * OWNED // rows_count
    sent_count = rows_count * pair_cap
    alive_slot = new_owner >= 0
    weights = jnp.where(
        alive_slot, jnp.where(block_pairs[0] == block_pairs[1], 1.0, 2.0), 0.0
    ).astype(jnp.float32)
    owner_rows = jnp.where(alive_slot, new_owner, rows_count)
    onehot = (owner_rows[:, None] == jnp.arange(rows_count, dtype=jnp.int32)[None, :]).astype(
        jnp.int32
    )
    ranking = jnp.sum(jnp.cumsum(onehot, axis=0) * onehot, axis=1) - 1
    placing = jnp.where(alive_slot, owner_rows * pair_cap + ranking, sent_count)
    slot_table = (
        jnp.full((sent_count,), held_slots, jnp.int32)
        .at[placing]
        .set(jnp.arange(held_slots, dtype=jnp.int32), mode="drop")
    )
    chosen = jnp.minimum(slot_table, held_slots - 1)
    sent_weights = jnp.where(slot_table < held_slots, weights[chosen], 0.0).astype(jnp.bfloat16)
    partial_correlation = slot_correlation(residuals, weights)
    correlation = lax.psum(partial_correlation, ("rows", "cols"))
    solved = small_solve(correlation, jnp.ones((correlation.shape[0],), jnp.float32))
    coefficients = solved / jnp.sum(solved)
    mixed_blocks = blend_history(densities, residuals, coefficients)
    arrived = (
        lax.all_to_all(
            jnp.take(mixed_blocks, chosen, axis=0), "rows", split_axis=0, concat_axis=0, tiled=True
        ),
        lax.all_to_all(sent_weights, "rows", split_axis=0, concat_axis=0, tiled=True),
    )
    ordering = compact_order(arrived[1].astype(jnp.float32))
    owned_blocks = jnp.take(arrived[0], ordering, axis=0)
    return (owned_blocks, coefficients)


def solution(mesh):
    return jax.shard_map(
        on_device,
        mesh=mesh,
        in_specs=(
            P(None, ("rows", "cols"), None, None),
            P(None, ("rows", "cols"), None, None),
            P(None, ("rows", "cols")),
            P(("rows", "cols")),
        ),
        out_specs=(P(("rows", "cols"), None, None), P()),
        check_vma=False,
    )
```

profile of v0, /device:TPU:0, one launch (start us, length us, event | category | flops | bytes accessed | tf_op | source)
XLA Modules:
  0.0 206.4 jit_solution(422986067294150492)
XLA Ops:
  0.6 0.7 compare_select_fusion.8
  1.3 0.8 compare_select_fusion.6
  2.1 0.1 reduce_window_sum.18
  2.2 0.2 select_reduce_fusion
  2.4 0.7 compare_select_fusion.3
  3.1 0.8 scatter_custom_fusion
  3.9 0.8 gather_fusion
  4.7 0.7 all_to_all.12
  5.4 7.3 %all-to-all-start = ((bf16[8,8,1]{1,2,0:T(2,128)(2,1)}), bf16[8,8,1]{1,2,0:T(2,128)(2,1)S(1)}, u32[]{:S(2)}, u32[]{:S(2)}) async-start(bf16[8,8,1]{1,2,0:T(2,128)(2,1)} %all_to_all.12), calls=%async_computation | async-start | bytes 8192 | tf_op jit(solution)/shard_map/all_to_all | solution.py:88
  12.6 19.3 %reshape.301 = bf16[6,64,16384]{2,1,0:T(8,128)(2,1)} reshape(bf16[6,64,128,128]{3,2,1,0:T(8,128)(2,1)} %param.17) | data formatting | bytes 25165824 | tf_op jit(solution)/shard_map/reshape | solution.py:30
  32.0 25.8 %fusion = bf16[64,6,6]{2,1,0:T(8,128)(2,1)S(1)} fusion(bf16[6,64,16384]{2,1,0:T(8,128)(2,1)} %reshape.301), kind=kOutput, calls=%fused_computation.5 | convolution fusion | flops 75497472 | bytes 12587520 | tf_op jit(solution)/shard_map/isn,ksn->sik/dot_general | solution.py:31
  57.7 0.1 fusion.3
  57.9 40.9 %psum.7 = f32[6,6]{1,0:T(8,128)S(1)} all-reduce(f32[6,6]{1,0:T(8,128)S(1)} %bitcast.83), channel_id=1, replica_groups=mesh['rows'=8,'cols'=4] {'rows','cols'}, use_global_device_ids=true, to_apply=%region_5.6 | all-reduce | flops 36 | bytes 288 | tf_op jit(solution)/shard_map/psum | solution.py:80
  98.8 0.5 slice.245
  99.3 0.8 fusion.7
  100.1 0.6 slice.248
  100.7 0.8 select_reduce_fusion.5
  101.6 0.1 multiply_subtract_fusion.4
  101.6 0.6 slice.252
  102.2 0.8 select_reduce_fusion.4
  103.1 0.1 multiply_subtract_fusion.3
  103.1 0.6 slice.256
  103.7 0.8 select_reduce_fusion.3
  104.6 0.1 multiply_subtract_fusion.2
  104.6 0.6 slice.260
  105.2 0.8 select_reduce_fusion.2
  106.1 0.1 multiply_subtract_fusion.1
  106.1 0.6 slice.264
  106.7 0.8 select_reduce_fusion.1
  107.6 0.1 multiply_subtract_fusion
  107.6 0.7 fusion.29
  108.3 0.6 fusion.37
  108.9 0.6 slice.249
  109.5 0.6 fusion.16
  110.2 0.6 slice.253
  110.8 0.6 fusion.19
  111.4 0.6 slice.257
  112.0 0.6 fusion.22
  112.7 0.6 slice.261
  113.2 0.6 fusion.25
  113.9 0.6 slice.265
  114.5 0.6 fusion.28
  115.1 0.7 fusion.39
  117.7 0.7 fusion.26
  120.3 0.6 fusion.23
  122.8 0.6 fusion.20
  125.3 0.6 fusion.17
  127.9 0.6 fusion.14
  130.4 0.6 reduce_sum.79
  131.0 0.6 broadcast_divide_fusion
  131.7 0.7 fusion.38
  132.3 16.1 %fusion.2 = bf16[64,128,128]{2,1,0:T(8,128)(2,1)} fusion(bf16[6,64,128,128]{3,2,1,0:T(8,128)(2,1)} %param.17, bf16[6,64,128,128]{3,2,1,0:T(8,128)(2,1)} %param.16, f32[]{:T(128)} %bitcast.49, f32[]{:T(128)} %bitcast.48, f32[]{:T(128)} %bitcast.47, f32[]{:T(128)} %bitcast.46, f32[]{:T(128)} %bitcast.45, f32[]{:T(128)} %bitcast.44), kind=kLoop, calls=%fused_computation.9 | loop fusion | flops 37748736 | bytes 27263000 | tf_op jit(solution)/shard_map/convert_element_type | solution.py:42
  148.4 2.5 %gather_fusion.1 = bf16[64,128,128]{2,1,0:T(8,128)(2,1)S(1)} fusion(bf16[64,128,128]{2,1,0:T(8,128)(2,1)} %fusion.2, s32[1024]{0:T(1024)S(1)} %pad_clamp_fusion.1), kind=kCustom, calls=%fused_computation.1 | custom fusion | bytes 4194560 | tf_op jit(solution)/shard_map/jit(_take)/gather | solution.py:86
  151.0 1.6 broadcast_select_fusion
  152.6 5.4 %all-to-all-start.1 = ((bf16[64,128,128]{2,1,0:T(8,128)(2,1)}), bf16[64,128,128]{2,1,0:T(8,128)(2,1)S(1)}, u32[]{:S(2)}, u32[]{:S(2)}) async-start(bf16[64,128,128]{2,1,0:T(8,128)(2,1)} %broadcast_select_fusion), calls=%async_computation.1 | async-start | bytes 4194304 | tf_op jit(solution)/shard_map/all_to_all | solution.py:85
  158.0 0.1 gt.109
  158.1 0.1 copy.17
  158.2 0.1 copy.16
  158.3 0.1 reduce-window.4
  158.4 0.1 fusion.5
  158.5 0.8 scatter_custom_fusion.1
  159.4 45.2 %all-to-all-done.1 = bf16[64,128,128]{2,1,0:T(8,128)(2,1)S(1)} async-done(((bf16[64,128,128]{2,1,0:T(8,128)(2,1)}), bf16[64,128,128]{2,1,0:T(8,128)(2,1)S(1)}, u32[]{:S(2)}, u32[]{:S(2)}) %all-to-all-start.1) | async-done | bytes 2097184 | tf_op jit(solution)/shard_map/all_to_all | solution.py:85
  204.6 0.7 gather_fusion.2
  205.3 1.1 broadcast_select_fusion.1
  (29 shorter events, 0.4 us)
Async XLA Ops:
  5.4 147.2 %all-to-all-start = ((bf16[8,8,1]{1,2,0:T(2,128)(2,1)}), bf16[8,8,1]{1,2,0:T(2,128)(2,1)S(1)}, u32[]{:S(2)}, u32[]{:S(2)}) async-start(bf16[8,8,1]{1,2,0:T(2,128)(2,1)} %all_to_all.12), calls=%async_computation | async-start | bytes 8192 | tf_op jit(solution)/shard_map/all_to_all | solution.py:88
  131.7 16.7 %copy-start = (f32[6]{0:T(128)}, f32[6]{0:T(128)S(1)}, u32[]{:S(2)}) copy-start(f32[6]{0:T(128)S(1)} %broadcast_divide_fusion) | copy-start | bytes 76
  152.6 52.0 %all-to-all-start.1 = ((bf16[64,128,128]{2,1,0:T(8,128)(2,1)}), bf16[64,128,128]{2,1,0:T(8,128)(2,1)S(1)}, u32[]{:S(2)}, u32[]{:S(2)}) async-start(bf16[64,128,128]{2,1,0:T(8,128)(2,1)} %broadcast_select_fusion), calls=%async_computation.1 | async-start | bytes 4194304 | tf_op jit(solution)/shard_map/all_to_all | solution.py:85
where the time goes:
time: 208 us; the launch traced here: 206 us
  waiting for transfers between devices  45.2 us (22%)
  blocking collectives  40.9 us (20%)
  other arithmetic  35.2 us (17%)
  local copies, waits for them, and re-layouts  34.4 us (17%)
  matrix products  25.9 us (12%)
  starting transfers between devices  12.7 us (6%)
  between operations  12.1 us (6%)
    all_to_all x1, waiting for transfers between devices, on_device(): lax.all_to_all(jnp.take(mixed_blocks, chosen, axis=0), 'rows', split_axis...  45.2 us
    psum x1, blocking collectives, on_device(): correlation = lax.psum(partial_correlation, ('rows', 'cols'))  40.9 us
    dot_general x1, matrix products, slot_correlation(): jnp.einsum('isn,ksn->sik', flattened, flattened, preferred_element_type=j...  25.8 us
    reshape x1, local copies, waits for them, and re-layouts, slot_correlation(): residual_set.reshape(residual_set.shape[0], residual_set.shape[1], -1)  19.3 us
    convert_element_type x1, other arithmetic, blend_history(): return running.astype(jnp.bfloat16)  16.1 us
    all_to_all x1, starting transfers between devices, on_device(): lax.all_to_all(sent_weights, 'rows', split_axis=0, concat_axis=0, tiled=T...  7.28 us
    all_to_all x1, starting transfers between devices, on_device(): lax.all_to_all(jnp.take(mixed_blocks, chosen, axis=0), 'rows', split_axis...  5.39 us
  transfers between devices with their start and end apart: 2, of which 1 were waited for; matrix products, arithmetic and copies ran while one was open for 43% of the time, Pallas kernels for 0%

commit v1 on v0

v1 whole, which is shorter than its diff:
```python
import functools

import jax
import jax.numpy as jnp
from jax import lax
from jax.experimental import pallas as pl
from jax.experimental.pallas import tpu as pltpu
from jax.sharding import PartitionSpec as P


OWNED = 32
LANES = 128
SUBLANES = 8
GRAM_SLOTS = 4
MIB = 1024 * 1024

mix_weight = 0.3


def pair_list(order_n):
    return [(i, k) for i in range(order_n) for k in range(i, order_n)]


def partner(index, step, count):
    return index ^ step if count & (count - 1) == 0 else lax.rem(index + step, count)


def pattern_of(owner, index, count):
    return owner ^ index if count & (count - 1) == 0 else lax.rem(owner + count - index, count)


def gram_kernel(rows_count, pair_cap, owner_ref, pairs_ref, residuals_ref, tile_ref, table_ref,
                held_ref, total_ref, weight_ref, count_ref, sems):
    order_n, held_slots = residuals_ref.shape[:2]
    chunks = held_slots // GRAM_SLOTS
    pairs = pair_list(order_n)
    my_row = lax.axis_index("rows")

    def chunk_copy(chunk):
        span = pl.ds(chunk * GRAM_SLOTS, GRAM_SLOTS)
        return pltpu.make_async_copy(residuals_ref.at[:, span], held_ref.at[:, span], sems.at[chunk])

    for chunk in range(chunks):
        chunk_copy(chunk).start()

    for row in range(rows_count):
        count_ref[row] = 0

    def clear(place, carry):
        table_ref[place] = 0
        return carry

    lax.fori_loop(0, rows_count * pair_cap, clear, 0, unroll=8)

    def route(slot, carry):
        owner = owner_ref[slot]
        alive = owner >= 0
        diagonal = pairs_ref[0, slot] == pairs_ref[1, slot]
        weight_ref[slot] = jnp.where(alive, jnp.where(diagonal, 1.0, 2.0), 0.0).astype(jnp.float32)

        @pl.when(alive)
        def _():
            rank = count_ref[owner]
            table_ref[pattern_of(owner, my_row, rows_count) * pair_cap + rank] = slot
            count_ref[owner] = rank + 1

        return carry

    lax.fori_loop(0, held_slots, route, 0, unroll=2)

    total_ref[...] = jnp.zeros_like(total_ref)
    groups = residuals_ref.shape[2] // (2 * SUBLANES)

    def slot_step(slot, carry):
        sums = [None] * len(pairs)
        for group in range(groups):
            rows = pl.ds(group * 2 * SUBLANES, 2 * SUBLANES)
            wide = [held_ref[i, slot, rows, :].astype(jnp.float32) for i in range(order_n)]
            for half in range(2):
                part = [x[half * SUBLANES:(half + 1) * SUBLANES] for x in wide]
                for e, (i, k) in enumerate(pairs):
                    product = part[i] * part[k]
                    sums[e] = product if sums[e] is None else sums[e] + product
        weight = weight_ref[slot]
        for e in range(len(pairs)):
            total_ref[e] += weight * sums[e]
        return carry

    for chunk in range(chunks):
        chunk_copy(chunk).wait()
        lax.fori_loop(chunk * GRAM_SLOTS, (chunk + 1) * GRAM_SLOTS, slot_step, 0)

    lanes = lax.broadcasted_iota(jnp.int32, (1, LANES), 1)
    entry_row = jnp.zeros((1, LANES), jnp.float32)
    for e in range(len(pairs)):
        entry = jnp.sum(jnp.sum(total_ref[e], axis=0, keepdims=True), axis=1, keepdims=True)
        entry_row = jnp.where(lanes == e, entry, entry_row)
    count_row = jnp.zeros((1, LANES), jnp.float32)
    for row in range(rows_count):
        count_row = jnp.where(lanes == row, count_ref[row].astype(jnp.float32), count_row)
    rows = lax.broadcasted_iota(jnp.int32, (SUBLANES, LANES), 0)
    tile = jnp.where(rows == 0, entry_row, jnp.where(rows == 1, count_row, 0.0))
    tile_ref[...] = jnp.broadcast_to(tile[None], tile_ref.shape)


def gram_call(residuals, block_pairs, new_owner, rows_count, device_count, pair_cap):
    order_n, held_slots = residuals.shape[:2]
    return pl.pallas_call(
        functools.partial(gram_kernel, rows_count, pair_cap),
        out_shape=(
            jax.ShapeDtypeStruct((device_count, SUBLANES, LANES), jnp.float32),
            jax.ShapeDtypeStruct((rows_count * pair_cap,), jnp.int32),
        ),
        in_specs=[
            pl.BlockSpec(memory_space=pltpu.SMEM),
            pl.BlockSpec(memory_space=pltpu.SMEM),
            pl.BlockSpec(memory_space=pltpu.HBM),
        ],
        out_specs=(
            pl.BlockSpec(memory_space=pltpu.VMEM),
            pl.BlockSpec(memory_space=pltpu.SMEM),
        ),
        scratch_shapes=[
            pltpu.VMEM(residuals.shape, residuals.dtype),
            pltpu.VMEM((len(pair_list(order_n)), SUBLANES, LANES), jnp.float32),
            pltpu.SMEM((held_slots,), jnp.float32),
            pltpu.SMEM((rows_count,), jnp.int32),
            pltpu.SemaphoreType.DMA((held_slots // GRAM_SLOTS,)),
        ],
        compiler_params=pltpu.CompilerParams(vmem_limit_bytes=20 * MIB),
        name="gram",
    )(new_owner, block_pairs, residuals)


def solve_rows(total, order_n):
    entry = {}
    for e, (i, k) in enumerate(pair_list(order_n)):
        entry[i, k] = jnp.broadcast_to(total[0:1, e:e + 1], (SUBLANES, LANES))
    vector = [jnp.ones((SUBLANES, LANES), jnp.float32)] * order_n
    for step in range(order_n):
        for i in range(step + 1, order_n):
            factor = entry[step, i] / entry[step, step]
            for k in range(i, order_n):
                entry[i, k] = entry[i, k] - factor * entry[step, k]
            vector[i] = vector[i] - factor * vector[step]
    solved = [None] * order_n
    for step in reversed(range(order_n)):
        inner = vector[step]
        for k in range(step + 1, order_n):
            inner = inner - entry[step, k] * solved[k]
        solved[step] = inner / entry[step, step]
    whole = functools.reduce(jnp.add, solved)
    return [x / whole for x in solved]


def blend_kernel(solving, step, pair_cap, table_ref, head_ref, densities_ref, residuals_ref, *rest):
    if solving:
        mixed_ref, coef_ref, density_ref, residual_ref, sems = rest
    else:
        mixed_ref, density_ref, residual_ref, sems = rest
    order_n = densities_ref.shape[0]

    def copies(place):
        slot = table_ref[step * pair_cap + place]
        return (
            pltpu.make_async_copy(densities_ref.at[:, slot], density_ref.at[:, place], sems.at[0, place]),
            pltpu.make_async_copy(residuals_ref.at[:, slot], residual_ref.at[:, place], sems.at[1, place]),
        )

    for place in range(pair_cap):
        for copy in copies(place):
            copy.start()
    if solving:
        coefs = solve_rows(jnp.sum(head_ref[...], axis=0), order_n)
        rows = lax.broadcasted_iota(jnp.int32, (SUBLANES, LANES), 0)
        stacked = jnp.zeros((SUBLANES, LANES), jnp.float32)
        for i in range(order_n):
            stacked = jnp.where(rows == i, coefs[i], stacked)
        coef_ref[...] = stacked
    else:
        coefs = [jnp.broadcast_to(head_ref[i:i + 1, :], (SUBLANES, LANES)) for i in range(order_n)]
    coefs = [jnp.concatenate([c, c], axis=0) for c in coefs]
    groups = mixed_ref.shape[1] // (2 * SUBLANES)
    for place in range(pair_cap):
        for copy in copies(place):
            copy.wait()
        for group in range(groups):
            rows = pl.ds(group * 2 * SUBLANES, 2 * SUBLANES)
            running = None
            for i in range(order_n):
                term = coefs[i] * (
                    density_ref[i, place, rows, :].astype(jnp.float32)
                    + mix_weight * residual_ref[i, place, rows, :].astype(jnp.float32)
                )
                running = term if running is None else running + term
            mixed_ref[place, rows, :] = running.astype(mixed_ref.dtype)


def blend_call(solving, step, pair_cap, table, head, densities, residuals):
    order_n = densities.shape[0]
    block = densities.shape[2:]
    mixed = pltpu.VMEM((pair_cap,) + block, jnp.bfloat16)
    coef = jax.ShapeDtypeStruct((SUBLANES, LANES), jnp.float32)
    vmem = pl.BlockSpec(memory_space=pltpu.VMEM)
    return pl.pallas_call(
        functools.partial(blend_kernel, solving, step, pair_cap),
        out_shape=(mixed, coef) if solving else mixed,
        in_specs=[
            pl.BlockSpec(memory_space=pltpu.SMEM),
            vmem,
            pl.BlockSpec(memory_space=pltpu.HBM),
            pl.BlockSpec(memory_space=pltpu.HBM),
        ],
        out_specs=(vmem, vmem) if solving else vmem,
        scratch_shapes=[
            pltpu.VMEM((order_n, pair_cap) + block, densities.dtype),
            pltpu.VMEM((order_n, pair_cap) + block, residuals.dtype),
            pltpu.SemaphoreType.DMA((2, pair_cap)),
        ],
        compiler_params=pltpu.CompilerParams(vmem_limit_bytes=8 * MIB),
    )(table, head, densities, residuals)


def place_kernel(rows_count, pair_cap, count_ref, offset_ref, *rest):
    arrived = rest[:rows_count]
    owned_ref, sem = rest[rows_count:]

    def each(act):
        for step in range(rows_count):
            for place in range(pair_cap):

                @pl.when(place < count_ref[step])
                def _():
                    act(pltpu.make_async_copy(
                        arrived[step].at[place],
                        owned_ref.at[offset_ref[step] + place],
                        sem.at[step, place],
                    ))

    each(lambda copy: copy.start())
    each(lambda copy: copy.wait())


def place_call(counts, offsets, arrived):
    rows_count, pair_cap = len(arrived), arrived[0].shape[0]
    smem = pl.BlockSpec(memory_space=pltpu.SMEM)
    return pl.pallas_call(
        functools.partial(place_kernel, rows_count, pair_cap),
        out_shape=jax.ShapeDtypeStruct((OWNED,) + arrived[0].shape[1:], arrived[0].dtype),
        in_specs=[smem, smem] + [pl.BlockSpec(memory_space=pltpu.VMEM)] * rows_count,
        out_specs=pl.BlockSpec(memory_space=pl.ANY),
        scratch_shapes=[pltpu.SemaphoreType.DMA((rows_count, pair_cap))],
        compiler_params=pltpu.CompilerParams(vmem_limit_bytes=8 * MIB),
        name="place",
    )(counts, offsets, *[pltpu.with_memory_space_constraint(x, pltpu.VMEM) for x in arrived])


def step_order(rows_count):
    return [*range(rows_count // 2, rows_count), *range(1, rows_count // 2), 0]


def on_device(densities, residuals, block_pairs, new_owner):
    rows_count = lax.axis_size("rows")
    cols_count = lax.axis_size("cols")
    order_n = densities.shape[0]
    densities = pltpu.with_memory_space_constraint(densities, pltpu.HBM)
    residuals = pltpu.with_memory_space_constraint(residuals, pltpu.HBM)
    pair_cap = 2 * OWNED // rows_count
    my_row, my_col = lax.axis_index("rows"), lax.axis_index("cols")
    tiles, table = gram_call(
        residuals, block_pairs, new_owner, rows_count, rows_count * cols_count, pair_cap
    )
    tiles = lax.all_to_all(tiles, ("rows", "cols"), split_axis=0, concat_axis=0, tiled=True)

    arrived = [None] * rows_count
    head = pltpu.with_memory_space_constraint(tiles, pltpu.VMEM)
    coef = None
    for step in step_order(rows_count):
        if coef is None:
            mixed, coef = blend_call(True, step, pair_cap, table, head, densities, residuals)
        else:
            mixed = blend_call(False, step, pair_cap, table, coef, densities, residuals)
        if step:
            pairs = [(row, int(partner(row, step, rows_count))) for row in range(rows_count)]
            mixed = lax.ppermute(mixed, "rows", pairs)
        arrived[step] = mixed

    by_row = tiles.reshape(rows_count, cols_count, SUBLANES, LANES)[:, :, 1, :]
    by_row = lax.dynamic_index_in_dim(by_row, my_col, 1, keepdims=False)
    by_row = lax.dynamic_index_in_dim(by_row, my_row, 1, keepdims=False)
    row_ids = jnp.arange(rows_count, dtype=jnp.int32)
    from_row = row_ids ^ my_row if rows_count & (rows_count - 1) == 0 else (
        row_ids * -1 + my_row + rows_count) % rows_count
    counts = jnp.sum(jnp.where(from_row[:, None] == row_ids[None, :], by_row[None, :], 0.0), axis=1)
    offsets = jnp.sum(jnp.where(from_row[:, None] > row_ids[None, :], by_row[None, :], 0.0), axis=1)
    owned_blocks = place_call(counts.astype(jnp.int32), offsets.astype(jnp.int32), arrived)
    return (owned_blocks, coef[:order_n, 0])


def solution(mesh):
    return jax.shard_map(
        on_device,
        mesh=mesh,
        in_specs=(
            P(None, ("rows", "cols"), None, None),
            P(None, ("rows", "cols"), None, None),
            P(None, ("rows", "cols")),
            P(("rows", "cols")),
        ),
        out_specs=(P(("rows", "cols"), None, None), P()),
        check_vma=False,
    )
```

time: 208 us -> 103 us (0.50)
  other arithmetic: 35.2 us -> 0.2 us
  Pallas kernels: 0 us -> 33.5 us
  local copies, waits for them, and re-layouts: 34.4 us -> 2.13 us
  matrix products: 25.9 us -> 0 us
  blocking collectives: 40.9 us -> 15.3 us
  between operations: 12.1 us -> 0.73 us
  waiting for transfers between devices: 45.2 us -> 39.4 us
    all_to_all x2 -> x0, waiting for transfers between devices: 45.2 us -> none  [the longest x1 45.2 us: on_device(): lax.all_to_all(jnp.take(mixed_blocks, chosen, axis=0), 'rows', split_axis...]
    psum x1 -> x0, blocking collectives: 40.9 us -> none  [on_device(): correlation = lax.psum(partial_correlation, ('rows', 'cols'))]
    ppermute x0 -> x7, waiting for transfers between devices: none -> 39.4 us  [on_device(): mixed = lax.ppermute(mixed, 'rows', pairs)]
    pallas_call x0 -> x10, Pallas kernels: none -> 33.5 us  [the longest x8 21.8 us: blend_call(): pl.pallas_call(functools.partial(blend_kernel, solving, step, pair_cap),...]
    dot_general x2 -> x0, matrix products: 25.9 us -> none  [the longest x1 25.8 us: slot_correlation(): jnp.einsum('isn,ksn->sik', flattened, flattened, preferred_element_type=j...]
    reshape x1 -> x0, local copies, waits for them, and re-layouts: 19.3 us -> none  [slot_correlation(): residual_set.reshape(residual_set.shape[0], residual_set.shape[1], -1)]
    convert_element_type x4 -> x2, other arithmetic: 16.2 us -> 0.01 us  [the longest x1 0.01 us: on_device(): offsets.astype(jnp.int32)]
    all_to_all x0 -> x1, blocking collectives: none -> 15.3 us  [on_device(): lax.all_to_all(tiles, ('rows', 'cols'), split_axis=0, concat_axis=0, tile...]
  transfers between devices with their start and end apart: 2 -> 7, of which waited for: 1 -> 2; matrix products, arithmetic and copies ran while one was open for 43% -> 1% of each run, Pallas kernels for 0% -> 16%
where the time goes in v1:
time: 103 us
  waiting for transfers between devices  39.4 us (38%)
  Pallas kernels  33.5 us (33%)
  blocking collectives  15.3 us (15%)
  starting transfers between devices  11.3 us (11%)
  local copies, waits for them, and re-layouts  2.13 us (2%)
    ppermute x7, waiting for transfers between devices, on_device(): mixed = lax.ppermute(mixed, 'rows', pairs)  39.4 us
    pallas_call x8, Pallas kernels, blend_call(): pl.pallas_call(functools.partial(blend_kernel, solving, step, pair_cap),...  21.8 us
    all_to_all x1, blocking collectives, on_device(): lax.all_to_all(tiles, ('rows', 'cols'), split_axis=0, concat_axis=0, tile...  15.3 us
    ppermute x7, starting transfers between devices, on_device(): mixed = lax.ppermute(mixed, 'rows', pairs)  11.3 us
    pallas_call x1, Pallas kernels, gram_call(): pl.pallas_call(functools.partial(gram_kernel, rows_count, pair_cap), out_...  9.66 us
  transfers between devices with their start and end apart: 7, of which 2 were waited for; matrix products, arithmetic and copies ran while one was open for 1% of the time, Pallas kernels for 16%

profile of v1, /device:TPU:0, one launch (start us, length us, event | category | flops | bytes accessed | tf_op | source)
XLA Modules:
  0.0 102.6 jit_solution(13925477499594099548)
XLA Ops:
  0.6 0.0 copy-start
  0.6 0.7 copy-done
  1.3 0.0 copy-start.1
  1.3 0.7 copy-done.1
  2.0 9.7 %gram.1 = (f32[32,8,128]{2,1,0:T(8,128)S(1)}, s32[64]{0:T(128)S(1)}) custom-call(s32[64]{0:T(128)S(1)} %copy-done.1, s32[2,64]{1,0:T(2,128)S(1)} %copy-done, bf16[6,64,128,128]{3,2,1,0:T(8,128)(2,1)} %residuals_ref.17), custom_call_target="tpu_custom_call" | custom-call | tf_op jit(solution)/shard_map/gram/pallas_call | solution.py:108
  11.6 15.3 %all_to_all.5.head_ref = f32[32,8,128]{2,1,0:T(8,128)S(1)} all-to-all(f32[32,8,128]{2,1,0:T(8,128)S(1)} %get-tuple-element.6), channel_id=1, replica_groups=mesh['rows'=8,'cols'=4] {'rows','cols'}, dimensions={0} | all-to-all | bytes 262144 | tf_op jit(solution)/shard_map/all_to_all | solution.py:273
  27.0 2.8 %shard_map.59 = (bf16[8,128,128]{2,1,0:T(8,128)(2,1)S(1)}, f32[8,128]{1,0:T(8,128)S(1)}) custom-call(s32[64]{0:T(128)S(1)} %get-tuple-element.7.table_ref, f32[32,8,128]{2,1,0:T(8,128)S(1)} %all_to_all.5.head_ref, bf16[6,64,128,128]{3,2,1,0:T(8,128)(2,1)} %densities_ref.15, bf16[6,64,128,128]{3,2,1,0:T(8,128)(2,1)} %residuals_ref.17), custom_call_target="tpu_custom_call" | custom-call | tf_op jit(solution)/shard_map/pallas_call | solution.py:205
  29.8 2.7 %shard_map.61 = bf16[8,128,128]{2,1,0:T(8,128)(2,1)S(1)} custom-call(s32[64]{0:T(128)S(1)} %get-tuple-element.7.table_ref, f32[8,128]{1,0:T(8,128)S(1)} %get-tuple-element.8.head_ref, bf16[6,64,128,128]{3,2,1,0:T(8,128)(2,1)} %densities_ref.15, bf16[6,64,128,128]{3,2,1,0:T(8,128)(2,1)} %residuals_ref.17), custom_call_target="tpu_custom_call" | custom-call | tf_op jit(solution)/shard_map/pallas_call | solution.py:205
  32.5 1.3 %collective-permute-start = (bf16[8,128,128]{2,1,0:T(8,128)(2,1)S(1)}, bf16[8,128,128]{2,1,0:T(8,128)(2,1)S(1)}, u32[]{:S(2)}, u32[]{:S(2)}) collective-permute-start(bf16[8,128,128]{2,1,0:T(8,128)(2,1)S(1)} %shard_map.61), channel_id=1, source_target_pairs={{0,4},{4,0},{8,12},{12,8},{16,20},{20,16},{24,28},{28,24},{1,5},{5... | collective-permute-start | bytes 786440 | tf_op jit(solution)/shard_map/ppermute | solution.py:285
  33.9 2.7 %shard_map.62 = bf16[8,128,128]{2,1,0:T(8,128)(2,1)S(1)} custom-call(s32[64]{0:T(128)S(1)} %get-tuple-element.7.table_ref, f32[8,128]{1,0:T(8,128)S(1)} %get-tuple-element.8.head_ref, bf16[6,64,128,128]{3,2,1,0:T(8,128)(2,1)} %densities_ref.15, bf16[6,64,128,128]{3,2,1,0:T(8,128)(2,1)} %residuals_ref.17), custom_call_target="tpu_custom_call" | custom-call | tf_op jit(solution)/shard_map/pallas_call | solution.py:205
  36.6 1.3 %collective-permute-start.1 = (bf16[8,128,128]{2,1,0:T(8,128)(2,1)S(1)}, bf16[8,128,128]{2,1,0:T(8,128)(2,1)S(1)}, u32[]{:S(2)}, u32[]{:S(2)}) collective-permute-start(bf16[8,128,128]{2,1,0:T(8,128)(2,1)S(1)} %shard_map.62), channel_id=1, source_target_pairs={{0,8},{4,12},{8,0},{12,4},{16,24},{20,28},{24,16},{28,20},{1,9},{5... | collective-permute-start | bytes 786440 | tf_op jit(solution)/shard_map/ppermute | solution.py:285
  37.9 2.7 %shard_map.66 = bf16[8,128,128]{2,1,0:T(8,128)(2,1)S(1)} custom-call(s32[64]{0:T(128)S(1)} %get-tuple-element.7.table_ref, f32[8,128]{1,0:T(8,128)S(1)} %get-tuple-element.8.head_ref, bf16[6,64,128,128]{3,2,1,0:T(8,128)(2,1)} %densities_ref.15, bf16[6,64,128,128]{3,2,1,0:T(8,128)(2,1)} %residuals_ref.17), custom_call_target="tpu_custom_call" | custom-call | tf_op jit(solution)/shard_map/pallas_call | solution.py:205
  40.6 2.7 %shard_map.65 = bf16[8,128,128]{2,1,0:T(8,128)(2,1)S(1)} custom-call(s32[64]{0:T(128)S(1)} %get-tuple-element.7.table_ref, f32[8,128]{1,0:T(8,128)S(1)} %get-tuple-element.8.head_ref, bf16[6,64,128,128]{3,2,1,0:T(8,128)(2,1)} %densities_ref.15, bf16[6,64,128,128]{3,2,1,0:T(8,128)(2,1)} %residuals_ref.17), custom_call_target="tpu_custom_call" | custom-call | tf_op jit(solution)/shard_map/pallas_call | solution.py:205
  43.3 2.7 %shard_map.64 = bf16[8,128,128]{2,1,0:T(8,128)(2,1)S(1)} custom-call(s32[64]{0:T(128)S(1)} %get-tuple-element.7.table_ref, f32[8,128]{1,0:T(8,128)S(1)} %get-tuple-element.8.head_ref, bf16[6,64,128,128]{3,2,1,0:T(8,128)(2,1)} %densities_ref.15, bf16[6,64,128,128]{3,2,1,0:T(8,128)(2,1)} %residuals_ref.17), custom_call_target="tpu_custom_call" | custom-call | tf_op jit(solution)/shard_map/pallas_call | solution.py:205
  46.0 2.7 %shard_map.63 = bf16[8,128,128]{2,1,0:T(8,128)(2,1)S(1)} custom-call(s32[64]{0:T(128)S(1)} %get-tuple-element.7.table_ref, f32[8,128]{1,0:T(8,128)S(1)} %get-tuple-element.8.head_ref, bf16[6,64,128,128]{3,2,1,0:T(8,128)(2,1)} %densities_ref.15, bf16[6,64,128,128]{3,2,1,0:T(8,128)(2,1)} %residuals_ref.17), custom_call_target="tpu_custom_call" | custom-call | tf_op jit(solution)/shard_map/pallas_call | solution.py:205
  48.8 2.8 %collective-permute-start.2 = (bf16[8,128,128]{2,1,0:T(8,128)(2,1)S(1)}, bf16[8,128,128]{2,1,0:T(8,128)(2,1)S(1)}, u32[]{:S(2)}, u32[]{:S(2)}) collective-permute-start(bf16[8,128,128]{2,1,0:T(8,128)(2,1)S(1)} %shard_map.63), channel_id=1, source_target_pairs={{0,12},{4,8},{8,4},{12,0},{16,28},{20,24},{24,20},{28,16},{1,13},{... | collective-permute-start | bytes 786440 | tf_op jit(solution)/shard_map/ppermute | solution.py:285
  51.6 1.8 %collective-permute-start.4 = (bf16[8,128,128]{2,1,0:T(8,128)(2,1)S(1)}, bf16[8,128,128]{2,1,0:T(8,128)(2,1)S(1)}, u32[]{:S(2)}, u32[]{:S(2)}) collective-permute-start(bf16[8,128,128]{2,1,0:T(8,128)(2,1)S(1)} %shard_map.64), channel_id=1, source_target_pairs={{0,20},{4,16},{8,28},{12,24},{16,4},{20,0},{24,12},{28,8},{1,21},{... | collective-permute-start | bytes 786440 | tf_op jit(solution)/shard_map/ppermute | solution.py:285
  53.3 0.8 collective-permute-start.5
  54.1 0.0 collective-permute-done.rest_1_
  54.1 3.0 %collective-permute-start.6 = (bf16[8,128,128]{2,1,0:T(8,128)(2,1)S(1)}, bf16[8,128,128]{2,1,0:T(8,128)(2,1)S(1)}, u32[]{:S(2)}, u32[]{:S(2)}) collective-permute-start(bf16[8,128,128]{2,1,0:T(8,128)(2,1)S(1)} %shard_map.66), channel_id=1, source_target_pairs={{0,28},{4,24},{8,20},{12,16},{16,12},{20,8},{24,4},{28,0},{1,29},{... | collective-permute-start | bytes 786440 | tf_op jit(solution)/shard_map/ppermute | solution.py:285
  57.1 0.0 collective-permute-done.1.rest_2_
  57.1 0.3 collective-permute-start.3
  57.4 0.1 constant_dynamic-slice_fusion
  57.5 2.7 %shard_map.60.rest_0_ = bf16[8,128,128]{2,1,0:T(8,128)(2,1)S(1)} custom-call(s32[64]{0:T(128)S(1)} %get-tuple-element.7.table_ref, f32[8,128]{1,0:T(8,128)S(1)} %get-tuple-element.8.head_ref, bf16[6,64,128,128]{3,2,1,0:T(8,128)(2,1)} %densities_ref.15, bf16[6,64,128,128]{3,2,1,0:T(8,128)(2,1)} %residuals_ref.17), custom_call_target="tpu_custom_call" | custom-call | tf_op jit(solution)/shard_map/pallas_call | solution.py:205
  60.2 0.1 copy.10
  60.3 0.2 select_reduce_fusion
  60.5 0.6 slice_reduce_fusion
  61.1 0.0 collective-permute-done.2.rest_3_
  61.1 23.3 %collective-permute-done.4.rest_5_ = bf16[8,128,128]{2,1,0:T(8,128)(2,1)S(1)} collective-permute-done((bf16[8,128,128]{2,1,0:T(8,128)(2,1)S(1)}, bf16[8,128,128]{2,1,0:T(8,128)(2,1)S(1)}, u32[]{:S(2)}, u32[]{:S(2)}) %collective-permute-start.4) | collective-permute-done | bytes 262176 | tf_op jit(solution)/shard_map/ppermute | solution.py:285
  84.4 0.0 collective-permute-done.5.rest_6_
  84.4 0.0 collective-permute-done.6.rest_7_
  84.5 16.1 %collective-permute-done.3.rest_4_ = bf16[8,128,128]{2,1,0:T(8,128)(2,1)S(1)} collective-permute-done((bf16[8,128,128]{2,1,0:T(8,128)(2,1)S(1)}, bf16[8,128,128]{2,1,0:T(8,128)(2,1)S(1)}, u32[]{:S(2)}, u32[]{:S(2)}) %collective-permute-start.3) | collective-permute-done | bytes 262176 | tf_op jit(solution)/shard_map/ppermute | solution.py:285
  100.6 2.1 %place.1 = bf16[32,128,128]{2,1,0:T(8,128)(2,1)} custom-call(s32[8]{0:T(128)S(1)} %convert_element_type.6.count_ref, s32[8]{0:T(128)S(1)} %convert_element_type.7.offset_ref, bf16[8,128,128]{2,1,0:T(8,128)(2,1)S(1)} %shard_map.60.rest_0_, bf16[8,128,128]{2,1,0:T(8,128)(2,1)S(1)} %collective-permute-done.rest_1_, ...), custom_call_target="tpu_custom_call" | custom-call | tf_op jit(solution)/shard_map/place/pallas_call | solution.py:247
  (4 shorter events, 0.0 us)
Async XLA Ops:
  0.6 0.7 copy-start
  1.3 0.7 copy-start.1
  32.5 21.6 %collective-permute-start = (bf16[8,128,128]{2,1,0:T(8,128)(2,1)S(1)}, bf16[8,128,128]{2,1,0:T(8,128)(2,1)S(1)}, u32[]{:S(2)}, u32[]{:S(2)}) collective-permute-start(bf16[8,128,128]{2,1,0:T(8,128)(2,1)S(1)} %shard_map.61), channel_id=1, source_target_pairs={{0,4},{4,0},{8,12},{12,8},{16,20},{20,16},{24,28},{28,24},{1,5},{5... | collective-permute-start | bytes 786440 | tf_op jit(solution)/shard_map/ppermute | solution.py:285
  36.6 20.5 %collective-permute-start.1 = (bf16[8,128,128]{2,1,0:T(8,128)(2,1)S(1)}, bf16[8,128,128]{2,1,0:T(8,128)(2,1)S(1)}, u32[]{:S(2)}, u32[]{:S(2)}) collective-permute-start(bf16[8,128,128]{2,1,0:T(8,128)(2,1)S(1)} %shard_map.62), channel_id=1, source_target_pairs={{0,8},{4,12},{8,0},{12,4},{16,24},{20,28},{24,16},{28,20},{1,9},{5... | collective-permute-start | bytes 786440 | tf_op jit(solution)/shard_map/ppermute | solution.py:285
  48.8 12.4 %collective-permute-start.2 = (bf16[8,128,128]{2,1,0:T(8,128)(2,1)S(1)}, bf16[8,128,128]{2,1,0:T(8,128)(2,1)S(1)}, u32[]{:S(2)}, u32[]{:S(2)}) collective-permute-start(bf16[8,128,128]{2,1,0:T(8,128)(2,1)S(1)} %shard_map.63), channel_id=1, source_target_pairs={{0,12},{4,8},{8,4},{12,0},{16,28},{20,24},{24,20},{28,16},{1,13},{... | collective-permute-start | bytes 786440 | tf_op jit(solution)/shard_map/ppermute | solution.py:285
  51.6 32.9 %collective-permute-start.4 = (bf16[8,128,128]{2,1,0:T(8,128)(2,1)S(1)}, bf16[8,128,128]{2,1,0:T(8,128)(2,1)S(1)}, u32[]{:S(2)}, u32[]{:S(2)}) collective-permute-start(bf16[8,128,128]{2,1,0:T(8,128)(2,1)S(1)} %shard_map.64), channel_id=1, source_target_pairs={{0,20},{4,16},{8,28},{12,24},{16,4},{20,0},{24,12},{28,8},{1,21},{... | collective-permute-start | bytes 786440 | tf_op jit(solution)/shard_map/ppermute | solution.py:285
  53.3 31.1 %collective-permute-start.5 = (bf16[8,128,128]{2,1,0:T(8,128)(2,1)S(1)}, bf16[8,128,128]{2,1,0:T(8,128)(2,1)S(1)}, u32[]{:S(2)}, u32[]{:S(2)}) collective-permute-start(bf16[8,128,128]{2,1,0:T(8,128)(2,1)S(1)} %shard_map.65), channel_id=1, source_target_pairs={{0,24},{4,28},{8,16},{12,20},{16,8},{20,12},{24,0},{28,4},{1,25},{... | collective-permute-start | bytes 786440 | tf_op jit(solution)/shard_map/ppermute | solution.py:285
  54.1 30.3 %collective-permute-start.6 = (bf16[8,128,128]{2,1,0:T(8,128)(2,1)S(1)}, bf16[8,128,128]{2,1,0:T(8,128)(2,1)S(1)}, u32[]{:S(2)}, u32[]{:S(2)}) collective-permute-start(bf16[8,128,128]{2,1,0:T(8,128)(2,1)S(1)} %shard_map.66), channel_id=1, source_target_pairs={{0,28},{4,24},{8,20},{12,16},{16,12},{20,8},{24,4},{28,0},{1,29},{... | collective-permute-start | bytes 786440 | tf_op jit(solution)/shard_map/ppermute | solution.py:285
  57.1 43.5 %collective-permute-start.3 = (bf16[8,128,128]{2,1,0:T(8,128)(2,1)S(1)}, bf16[8,128,128]{2,1,0:T(8,128)(2,1)S(1)}, u32[]{:S(2)}, u32[]{:S(2)}) collective-permute-start(bf16[8,128,128]{2,1,0:T(8,128)(2,1)S(1)} %get-tuple-element.9), channel_id=1, source_target_pairs={{0,16},{4,20},{8,24},{12,28},{16,0},{20,4},{24,8},{28,12},{1,17},{... | collective-permute-start | bytes 786440 | tf_op jit(solution)/shard_map/ppermute | solution.py:285

commit v2 on v1

v2 whole, which is shorter than its diff:
```python
import functools

import jax
import jax.numpy as jnp
from jax import lax
from jax.experimental import pallas as pl
from jax.experimental.pallas import tpu as pltpu
from jax.sharding import PartitionSpec as P


OWNED = 32
LANES = 128
SUBLANES = 8
GRAM_SLOTS = 16
ROUTING = 2
TILE = 4
COUNT_LANE = 64
MIB = 1024 * 1024

mix_weight = 0.3


def pair_list(order_n):
    return [(i, k) for i in range(order_n) for k in range(i, order_n)]


def partner(index, step, count):
    return index ^ step if count & (count - 1) == 0 else lax.rem(index + step, count)


def pattern_of(owner, index, count):
    return owner ^ index if count & (count - 1) == 0 else lax.rem(owner + count - index, count)


def gram_kernel(rows_count, pair_cap, owner_hbm, pairs_hbm, residuals_ref, tile_ref, table_ref,
                held_ref, low_ref, high_ref, owner_ref, pairs_ref, count_ref, sems, index_sems):
    order_n, held_slots = residuals_ref.shape[:2]
    chunks = held_slots // GRAM_SLOTS
    pairs = pair_list(order_n)
    my_row = lax.axis_index("rows")
    sent_count = rows_count * pair_cap

    def chunk_copy(chunk):
        span = pl.ds(chunk * GRAM_SLOTS, GRAM_SLOTS)
        return pltpu.make_async_copy(residuals_ref.at[:, span], held_ref.at[:, span], sems.at[chunk])

    index_copies = (
        pltpu.make_async_copy(owner_hbm, owner_ref, index_sems.at[0]),
        pltpu.make_async_copy(pairs_hbm, pairs_ref, index_sems.at[1]),
    )
    for copy in index_copies:
        copy.start()
    for chunk in range(chunks):
        chunk_copy(chunk).start()

    for row in range(rows_count + 1):
        count_ref[row] = 0

    def clear(place, carry):
        table_ref[place] = 0
        return carry

    lax.fori_loop(0, sent_count, clear, 0, unroll=8)
    for ref in (low_ref, high_ref):
        ref[...] = jnp.zeros_like(ref)
    for copy in index_copies:
        copy.wait()

    def route(slot):
        owner = owner_ref[slot]
        alive = owner >= 0
        bucket = jnp.where(alive, owner, rows_count)
        rank = count_ref[bucket]
        count_ref[bucket] = rank + 1
        place = pattern_of(owner, my_row, rows_count) * pair_cap + rank
        table_ref[jnp.where(alive, place, sent_count)] = slot

    block_rows = residuals_ref.shape[2]
    half_rows = block_rows // 2

    def weight_of(slot):
        alive = owner_ref[slot] >= 0
        diagonal = pairs_ref[0, slot] == pairs_ref[1, slot]
        return jnp.where(alive, jnp.where(diagonal, 1.0, 2.0), 0.0).astype(jnp.float32)

    def matrix_slots(slots):
        plain = [
            jnp.concatenate(
                [held_ref[i, slot, pl.ds(start, half_rows), :] for slot in slots for start in (0, half_rows)],
                axis=1,
            )
            for i in range(order_n)
        ]
        weight = jnp.concatenate(
            [jnp.full((half_rows, 2 * LANES), weight_of(slot), jnp.float32).astype(jnp.bfloat16) for slot in slots],
            axis=1,
        )
        scaled = [x * weight for x in plain]
        for ref, span in ((low_ref, range(TILE)), (high_ref, range(TILE, order_n))):
            ref[...] += lax.dot_general(
                jnp.concatenate(scaled[span[0]:], axis=0),
                jnp.concatenate([plain[i] for i in span], axis=0),
                (((1,), (1,)), ((), ())),
                preferred_element_type=jnp.float32,
            )

    def chunk_step(routed, chunk, carry):
        chunk_copy(chunk).wait()
        for i in range(routed):
            route(chunk * routed + i)
        first_slot = chunk * GRAM_SLOTS
        matrix_slots([first_slot + i for i in range(GRAM_SLOTS)])
        return carry

    routing_chunks = chunks // ROUTING
    lax.fori_loop(0, routing_chunks, functools.partial(chunk_step, held_slots // routing_chunks), 0)
    lax.fori_loop(routing_chunks, chunks, functools.partial(chunk_step, 0), 0)

    lanes = lax.broadcasted_iota(jnp.int32, (1, LANES), 1)
    row = jnp.zeros((1, LANES), jnp.float32)
    for owner in range(rows_count):
        row = jnp.where(lanes == COUNT_LANE + owner, count_ref[owner].astype(jnp.float32), row)
    diagonals = {}
    for ref, span in ((low_ref, range(TILE)), (high_ref, range(TILE, order_n))):
        width = ref.shape[1]
        across = lax.broadcasted_iota(jnp.int32, (half_rows, width), 1)
        down = lax.broadcasted_iota(jnp.int32, (half_rows, width), 0)
        on_diagonal = across % half_rows == down
        for k in range(span[0], order_n):
            block = ref[pl.ds((k - span[0]) * half_rows, half_rows), :]
            line = jnp.sum(jnp.where(on_diagonal, block, 0.0), axis=0, keepdims=True)
            for i in span:
                if i <= k:
                    mine = across[0:1] // half_rows == i - span[0]
                    diagonals[i, k] = jnp.sum(jnp.where(mine, line, 0.0), axis=1, keepdims=True)
    for e, pair in enumerate(pairs):
        row = jnp.where(lanes == e, diagonals[pair], row)
    tile_ref[...] = jnp.broadcast_to(row[None], tile_ref.shape)


def gram_call(residuals, block_pairs, new_owner, rows_count, device_count, pair_cap):
    order_n, held_slots, block_rows = residuals.shape[:3]
    half_rows = block_rows // 2
    return pl.pallas_call(
        functools.partial(gram_kernel, rows_count, pair_cap),
        out_shape=(
            pltpu.VMEM((device_count, 1, LANES), jnp.float32),
            pltpu.SMEM((rows_count * pair_cap + 1,), jnp.int32),
        ),
        in_specs=[pl.BlockSpec(memory_space=pltpu.HBM)] * 3,
        out_specs=(pl.BlockSpec(memory_space=pltpu.VMEM), pl.BlockSpec(memory_space=pltpu.SMEM)),
        scratch_shapes=[
            pltpu.VMEM(residuals.shape, residuals.dtype),
            pltpu.VMEM((order_n * half_rows, TILE * half_rows), jnp.float32),
            pltpu.VMEM(((order_n - TILE) * half_rows,) * 2, jnp.float32),
            pltpu.SMEM(new_owner.shape, jnp.int32),
            pltpu.SMEM(block_pairs.shape, jnp.int32),
            pltpu.SMEM((rows_count + 1,), jnp.int32),
            pltpu.SemaphoreType.DMA((held_slots // GRAM_SLOTS,)),
            pltpu.SemaphoreType.DMA((2,)),
        ],
        compiler_params=pltpu.CompilerParams(vmem_limit_bytes=24 * MIB),
        name="gram",
    )(new_owner, block_pairs, residuals)


def solve_rows(total, order_n):
    entry = {}
    for e, (i, k) in enumerate(pair_list(order_n)):
        entry[i, k] = jnp.broadcast_to(total[0:1, e:e + 1], (SUBLANES, LANES))
    vector = [jnp.ones((SUBLANES, LANES), jnp.float32)] * order_n
    for step in range(order_n):
        for i in range(step + 1, order_n):
            factor = entry[step, i] / entry[step, step]
            for k in range(i, order_n):
                entry[i, k] = entry[i, k] - factor * entry[step, k]
            vector[i] = vector[i] - factor * vector[step]
    solved = [None] * order_n
    for step in reversed(range(order_n)):
        inner = vector[step]
        for k in range(step + 1, order_n):
            inner = inner - entry[step, k] * solved[k]
        solved[step] = inner / entry[step, step]
    whole = functools.reduce(jnp.add, solved)
    return [x / whole for x in solved]


def fetch_copies(step, pair_cap, table_ref, densities_ref, residuals_ref, density_ref, residual_ref, sems):
    def copies(place):
        slot = table_ref[step * pair_cap + place]
        return (
            pltpu.make_async_copy(densities_ref.at[:, slot], density_ref.at[:, place], sems.at[0, place]),
            pltpu.make_async_copy(residuals_ref.at[:, slot], residual_ref.at[:, place], sems.at[1, place]),
        )

    return copies


def row_groups(ref):
    return [pl.ds(start, 2 * SUBLANES) for start in range(0, ref.shape[-2], 2 * SUBLANES)]


def moved(density_ref, residual_ref, index):
    return density_ref[index].astype(jnp.float32) + mix_weight * residual_ref[index].astype(jnp.float32)


def prepare_kernel(step, pair_cap, table_ref, densities_ref, residuals_ref, moved_ref, density_ref, residual_ref, sems):
    copies = fetch_copies(step, pair_cap, table_ref, densities_ref, residuals_ref, density_ref, residual_ref, sems)
    for place in range(pair_cap):
        for copy in copies(place):
            copy.start()
    for place in range(pair_cap):
        for copy in copies(place):
            copy.wait()
        for rows in row_groups(moved_ref):
            for i in range(moved_ref.shape[0]):
                moved_ref[i, place, rows, :] = moved(density_ref, residual_ref, (i, place, rows, slice(None)))


def prepare_call(step, pair_cap, table, densities, residuals):
    shape = (densities.shape[0], pair_cap) + densities.shape[2:]
    hbm = pl.BlockSpec(memory_space=pltpu.HBM)
    return pl.pallas_call(
        functools.partial(prepare_kernel, step, pair_cap),
        out_shape=pltpu.VMEM(shape, jnp.float32),
        in_specs=[pl.BlockSpec(memory_space=pltpu.SMEM), hbm, hbm],
        out_specs=pl.BlockSpec(memory_space=pltpu.VMEM),
        scratch_shapes=[
            pltpu.VMEM(shape, densities.dtype),
            pltpu.VMEM(shape, residuals.dtype),
            pltpu.SemaphoreType.DMA((2, pair_cap)),
        ],
        compiler_params=pltpu.CompilerParams(vmem_limit_bytes=12 * MIB),
        name="prepare",
    )(pltpu.with_memory_space_constraint(table, pltpu.SMEM), densities, residuals)


def first_kernel(tiles_ref, moved_ref, mixed_ref, coef_ref):
    order_n = moved_ref.shape[0]
    total = tiles_ref[0]
    for device in range(1, tiles_ref.shape[0]):
        total = total + tiles_ref[device]
    coefs = solve_rows(total, order_n)
    rows = lax.broadcasted_iota(jnp.int32, (SUBLANES, LANES), 0)
    stacked = jnp.zeros((SUBLANES, LANES), jnp.float32)
    for i in range(order_n):
        stacked = jnp.where(rows == i, coefs[i], stacked)
    coef_ref[...] = stacked
    coefs = [jnp.concatenate([c, c], axis=0) for c in coefs]
    for place in range(mixed_ref.shape[0]):
        for rows in row_groups(mixed_ref):
            running = None
            for i, coef in enumerate(coefs):
                term = coef * moved_ref[i, place, rows, :]
                running = term if running is None else running + term
            mixed_ref[place, rows, :] = running.astype(mixed_ref.dtype)


def first_call(tiles, moved_blocks):
    vmem = pl.BlockSpec(memory_space=pltpu.VMEM)
    keep = functools.partial(pltpu.with_memory_space_constraint, memory_space=pltpu.VMEM)
    return pl.pallas_call(
        first_kernel,
        out_shape=(
            pltpu.VMEM(moved_blocks.shape[1:], jnp.bfloat16),
            pltpu.VMEM((SUBLANES, LANES), jnp.float32),
        ),
        in_specs=[vmem] * 2,
        out_specs=(vmem, vmem),
        compiler_params=pltpu.CompilerParams(vmem_limit_bytes=8 * MIB),
        name="blend_first",
    )(keep(tiles), keep(moved_blocks))


def blend_kernel(step, pair_cap, table_ref, coef_ref, densities_ref, residuals_ref,
                 mixed_ref, density_ref, residual_ref, sems):
    order_n = densities_ref.shape[0]
    copies = fetch_copies(step, pair_cap, table_ref, densities_ref, residuals_ref, density_ref, residual_ref, sems)
    for place in range(pair_cap):
        for copy in copies(place):
            copy.start()
    coefs = [jnp.broadcast_to(coef_ref[i:i + 1, :], (2 * SUBLANES, LANES)) for i in range(order_n)]
    for place in range(pair_cap):
        for copy in copies(place):
            copy.wait()
        for rows in row_groups(mixed_ref):
            running = None
            for i, coef in enumerate(coefs):
                term = coef * moved(density_ref, residual_ref, (i, place, rows, slice(None)))
                running = term if running is None else running + term
            mixed_ref[place, rows, :] = running.astype(mixed_ref.dtype)


def blend_call(step, pair_cap, table, coef, densities, residuals):
    order_n = densities.shape[0]
    block = densities.shape[2:]
    vmem = pl.BlockSpec(memory_space=pltpu.VMEM)
    hbm = pl.BlockSpec(memory_space=pltpu.HBM)
    return pl.pallas_call(
        functools.partial(blend_kernel, step, pair_cap),
        out_shape=pltpu.VMEM((pair_cap,) + block, jnp.bfloat16),
        in_specs=[pl.BlockSpec(memory_space=pltpu.SMEM), vmem, hbm, hbm],
        out_specs=vmem,
        scratch_shapes=[
            pltpu.VMEM((order_n, pair_cap) + block, densities.dtype),
            pltpu.VMEM((order_n, pair_cap) + block, residuals.dtype),
            pltpu.SemaphoreType.DMA((2, pair_cap)),
        ],
        compiler_params=pltpu.CompilerParams(vmem_limit_bytes=8 * MIB),
    )(
        pltpu.with_memory_space_constraint(table, pltpu.SMEM),
        pltpu.with_memory_space_constraint(coef, pltpu.VMEM),
        densities,
        residuals,
    )


def place_kernel(steps, count_ref, offset_ref, *rest):
    arrived = rest[:len(steps)]
    owned_ref, sem = rest[-2:]

    def each(act):
        for n, step in enumerate(steps):
            count, offset = count_ref[step], offset_ref[step]
            size = arrived[n].shape[0]
            while size:
                before = count - lax.rem(count, 2 * size)

                @pl.when(lax.rem(count, 2 * size) >= size)
                def _():
                    act(pltpu.make_async_copy(
                        arrived[n].at[pl.ds(before, size)],
                        owned_ref.at[pl.ds(offset + before, size)],
                        sem.at[n, size.bit_length() - 1],
                    ))

                size //= 2

    each(lambda copy: copy.start())
    each(lambda copy: copy.wait())


def place_call(steps, counts, offsets, arrived, owned):
    pair_cap = arrived[0].shape[0]
    smem = pl.BlockSpec(memory_space=pltpu.SMEM)
    hbm = pl.BlockSpec(memory_space=pltpu.HBM)
    held = [pltpu.with_memory_space_constraint(x, pltpu.VMEM) for x in arrived]
    begun = [] if owned is None else [pltpu.with_memory_space_constraint(owned, pltpu.HBM)]
    return pl.pallas_call(
        functools.partial(place_kernel, steps),
        out_shape=pltpu.HBM((OWNED,) + arrived[0].shape[1:], arrived[0].dtype),
        in_specs=[smem, smem] + [pl.BlockSpec(memory_space=pltpu.VMEM)] * len(held) + [hbm] * len(begun),
        out_specs=hbm,
        scratch_shapes=[pltpu.SemaphoreType.DMA((len(held), pair_cap.bit_length()))],
        input_output_aliases={2 + len(held): 0} if begun else {},
        compiler_params=pltpu.CompilerParams(vmem_limit_bytes=4 * MIB),
        name="place",
    )(
        pltpu.with_memory_space_constraint(counts, pltpu.SMEM),
        pltpu.with_memory_space_constraint(offsets, pltpu.SMEM),
        *held,
        *begun,
    )


def step_order(rows_count):
    half = rows_count // 2
    far = [*range(half, rows_count)]
    near = [*range(half // 2, half), *range(1, half // 2)]
    return far[:half // 2] + near + far[half // 2:] + [0]


def on_device(densities, residuals, block_pairs, new_owner):
    rows_count = lax.axis_size("rows")
    cols_count = lax.axis_size("cols")
    order_n = densities.shape[0]
    densities = pltpu.with_memory_space_constraint(densities, pltpu.HBM)
    residuals = pltpu.with_memory_space_constraint(residuals, pltpu.HBM)
    pair_cap = 2 * OWNED // rows_count
    my_row, my_col = lax.axis_index("rows"), lax.axis_index("cols")
    order = step_order(rows_count)
    block_pairs = pltpu.with_memory_space_constraint(block_pairs, pltpu.HBM)
    new_owner = pltpu.with_memory_space_constraint(new_owner, pltpu.HBM)
    tiles, table = gram_call(
        residuals, block_pairs, new_owner, rows_count, rows_count * cols_count, pair_cap
    )
    tiles = lax.all_to_all(tiles, ("rows", "cols"), split_axis=0, concat_axis=0, tiled=True)
    moved_blocks = prepare_call(order[0], pair_cap, table, densities, residuals)

    arrived = [None] * rows_count
    coef = None
    for step in order:
        if coef is None:
            mixed, coef = first_call(tiles, moved_blocks)
        else:
            mixed = blend_call(step, pair_cap, table, coef, densities, residuals)
        if step:
            pairs = [(row, int(partner(row, step, rows_count))) for row in range(rows_count)]
            mixed = lax.ppermute(mixed, "rows", pairs)
        arrived[step] = mixed

    by_row = tiles.reshape(rows_count, cols_count, LANES)
    by_row = lax.dynamic_index_in_dim(by_row, my_col, 1, keepdims=False)
    by_row = lax.dynamic_index_in_dim(by_row, COUNT_LANE + my_row, 1, keepdims=False)
    row_ids = jnp.arange(rows_count, dtype=jnp.int32)
    from_row = row_ids ^ my_row if rows_count & (rows_count - 1) == 0 else (
        row_ids * -1 + my_row + rows_count) % rows_count
    counts = jnp.sum(jnp.where(from_row[:, None] == row_ids[None, :], by_row[None, :], 0.0), axis=1)
    offsets = jnp.sum(jnp.where(from_row[:, None] > row_ids[None, :], by_row[None, :], 0.0), axis=1)
    counts, offsets = counts.astype(jnp.int32), offsets.astype(jnp.int32)
    last = order[-2]
    early = [step for step in order if step != last]
    owned_blocks = place_call(early, counts, offsets, [arrived[step] for step in early], None)
    owned_blocks = place_call([last], counts, offsets, [arrived[last]], owned_blocks)
    return (owned_blocks, coef[:order_n, 0])


def solution(mesh):
    return jax.shard_map(
        on_device,
        mesh=mesh,
        in_specs=(
            P(None, ("rows", "cols"), None, None),
            P(None, ("rows", "cols"), None, None),
            P(None, ("rows", "cols")),
            P(("rows", "cols")),
        ),
        out_specs=(P(("rows", "cols"), None, None), P()),
        check_vma=False,
    )
```

time: 103 us -> 79.5 us (0.77)
  blocking collectives: 15.3 us -> 0 us
  waiting for transfers between devices: 39.4 us -> 29.2 us
  starting transfers between devices: 11.3 us -> 20.1 us
  Pallas kernels: 33.5 us -> 28 us
  local copies, waits for them, and re-layouts: 2.13 us -> 0.79 us
    all_to_all x1 -> x0, blocking collectives: 15.3 us -> none  [on_device(): lax.all_to_all(tiles, ('rows', 'cols'), split_axis=0, concat_axis=0, tile...]
    ppermute x7, waiting for transfers between devices: 39.4 us -> 24.3 us  [on_device(): mixed = lax.ppermute(mixed, 'rows', pairs)]
    all_to_all x0 -> x1, starting transfers between devices: none -> 7.33 us  [on_device(): lax.all_to_all(tiles, ('rows', 'cols'), split_axis=0, concat_axis=0, tile...]
    all_to_all x0 -> x1, waiting for transfers between devices: none -> 4.96 us  [on_device(): lax.all_to_all(tiles, ('rows', 'cols'), split_axis=0, concat_axis=0, tile...]
    pallas_call x9 -> x11, Pallas kernels: 23.8 us -> 20 us  [the longest x7 15.1 us: blend_call(): pl.pallas_call(functools.partial(blend_kernel, step, pair_cap), out_shape...]
    pallas_call x1, Pallas kernels: 9.66 us -> 7.93 us  [gram_call(): pl.pallas_call(functools.partial(gram_kernel, rows_count, pair_cap), out_...]
    ppermute x7, starting transfers between devices: 11.3 us -> 12.8 us  [on_device(): mixed = lax.ppermute(mixed, 'rows', pairs)]
    unnamed x5 -> x1, local copies, waits for them, and re-layouts: 1.41 us -> 0.08 us
  transfers between devices with their start and end apart: 7 -> 8, of which waited for: 2 -> 5; matrix products, arithmetic and copies ran while one was open for 1% -> 1% of each run, Pallas kernels for 16% -> 21%
where the time goes in v2:
time: 79.5 us; the launch traced here: 79 us
  waiting for transfers between devices  29.2 us (37%)
  Pallas kernels  28 us (35%)
  starting transfers between devices  20.1 us (25%)
    ppermute x7, waiting for transfers between devices, on_device(): mixed = lax.ppermute(mixed, 'rows', pairs)  24.3 us
    pallas_call x7, Pallas kernels, blend_call(): pl.pallas_call(functools.partial(blend_kernel, step, pair_cap), out_shape...  15.1 us
    ppermute x7, starting transfers between devices, on_device(): mixed = lax.ppermute(mixed, 'rows', pairs)  12.8 us
    pallas_call x1, Pallas kernels, gram_call(): pl.pallas_call(functools.partial(gram_kernel, rows_count, pair_cap), out_...  7.93 us
    all_to_all x1, starting transfers between devices, on_device(): lax.all_to_all(tiles, ('rows', 'cols'), split_axis=0, concat_axis=0, tile...  7.33 us
    all_to_all x1, waiting for transfers between devices, on_device(): lax.all_to_all(tiles, ('rows', 'cols'), split_axis=0, concat_axis=0, tile...  4.96 us
    pallas_call x2, Pallas kernels, place_call(): pl.pallas_call(functools.partial(place_kernel, steps), out_shape=pltpu.HB...  2.36 us
    pallas_call x1, Pallas kernels, prepare_call(): pl.pallas_call(functools.partial(prepare_kernel, step, pair_cap), out_sha...  2.14 us
  transfers between devices with their start and end apart: 8, of which 5 were waited for; matrix products, arithmetic and copies ran while one was open for 1% of the time, Pallas kernels for 21%

profile of v2, /device:TPU:0, one launch (start us, length us, event | category | flops | bytes accessed | tf_op | source)
XLA Modules:
  0.0 79.0 jit_solution(5698995233354778110)
XLA Ops:
  0.6 7.9 %gram.1 = (f32[32,1,128]{2,1,0:T(1,128)}, s32[65]{0:T(128)S(4)}) custom-call(s32[64]{0:T(128)} %owner_hbm.1, s32[2,64]{1,0:T(2,128)} %pairs_hbm.1, bf16[6,64,128,128]{3,2,1,0:T(8,128)(2,1)} %residuals_ref.17), custom_call_target="tpu_custom_call" | custom-call | tf_op jit(solution)/shard_map/gram/pallas_call | solution.py:144
  8.6 7.3 %all-to-all-start = ((f32[32,1,128]{2,1,0:T(1,128)}), f32[32,1,128]{2,1,0:T(1,128)S(1)}, u32[]{:S(2)}, u32[]{:S(2)}) async-start(f32[32,1,128]{2,1,0:T(1,128)} %get-tuple-element.6), calls=%async_computation | async-start | bytes 32768 | tf_op jit(solution)/shard_map/all_to_all | solution.py:387
  15.9 2.1 %prepare.1.moved_ref = f32[6,8,128,128]{3,2,1,0:T(8,128)S(1)} custom-call(s32[65]{0:T(128)S(4)} %get-tuple-element.7.table_ref, bf16[6,64,128,128]{3,2,1,0:T(8,128)(2,1)} %densities_ref.15, bf16[6,64,128,128]{3,2,1,0:T(8,128)(2,1)} %residuals_ref.17), custom_call_target="tpu_custom_call" | custom-call | tf_op jit(solution)/shard_map/prepare/pallas_call | solution.py:223
  18.0 5.0 %all-to-all-done.tiles_ref = f32[32,1,128]{2,1,0:T(1,128)S(1)} async-done(((f32[32,1,128]{2,1,0:T(1,128)}), f32[32,1,128]{2,1,0:T(1,128)S(1)}, u32[]{:S(2)}, u32[]{:S(2)}) %all-to-all-start) | async-done | bytes 16416 | tf_op jit(solution)/shard_map/all_to_all | solution.py:387
  23.0 0.4 blend_first.1
  23.4 2.2 %shard_map.60 = bf16[8,128,128]{2,1,0:T(8,128)(2,1)S(1)} custom-call(s32[65]{0:T(128)S(4)} %get-tuple-element.7.table_ref, f32[8,128]{1,0:T(8,128)S(1)} %get-tuple-element.8.coef_ref, bf16[6,64,128,128]{3,2,1,0:T(8,128)(2,1)} %densities_ref.15, bf16[6,64,128,128]{3,2,1,0:T(8,128)(2,1)} %residuals_ref.17), custom_call_target="tpu_custom_call" | custom-call | tf_op jit(solution)/shard_map/pallas_call | solution.py:299
  25.6 0.7 collective-permute-start.2
  26.2 2.2 %shard_map.61 = bf16[8,128,128]{2,1,0:T(8,128)(2,1)S(1)} custom-call(s32[65]{0:T(128)S(4)} %get-tuple-element.7.table_ref, f32[8,128]{1,0:T(8,128)S(1)} %get-tuple-element.8.coef_ref, bf16[6,64,128,128]{3,2,1,0:T(8,128)(2,1)} %densities_ref.15, bf16[6,64,128,128]{3,2,1,0:T(8,128)(2,1)} %residuals_ref.17), custom_call_target="tpu_custom_call" | custom-call | tf_op jit(solution)/shard_map/pallas_call | solution.py:299
  28.4 1.2 %collective-permute-start.3 = (bf16[8,128,128]{2,1,0:T(8,128)(2,1)S(1)}, bf16[8,128,128]{2,1,0:T(8,128)(2,1)S(1)}, u32[]{:S(2)}, u32[]{:S(2)}) collective-permute-start(bf16[8,128,128]{2,1,0:T(8,128)(2,1)S(1)} %shard_map.61), channel_id=1, source_target_pairs={{0,8},{4,12},{8,0},{12,4},{16,24},{20,28},{24,16},{28,20},{1,9},{5... | collective-permute-start | bytes 786440 | tf_op jit(solution)/shard_map/ppermute | solution.py:399
  29.6 2.2 %shard_map.64 = bf16[8,128,128]{2,1,0:T(8,128)(2,1)S(1)} custom-call(s32[65]{0:T(128)S(4)} %get-tuple-element.7.table_ref, f32[8,128]{1,0:T(8,128)S(1)} %get-tuple-element.8.coef_ref, bf16[6,64,128,128]{3,2,1,0:T(8,128)(2,1)} %densities_ref.15, bf16[6,64,128,128]{3,2,1,0:T(8,128)(2,1)} %residuals_ref.17), custom_call_target="tpu_custom_call" | custom-call | tf_op jit(solution)/shard_map/pallas_call | solution.py:299
  31.7 2.2 %shard_map.63 = bf16[8,128,128]{2,1,0:T(8,128)(2,1)S(1)} custom-call(s32[65]{0:T(128)S(4)} %get-tuple-element.7.table_ref, f32[8,128]{1,0:T(8,128)S(1)} %get-tuple-element.8.coef_ref, bf16[6,64,128,128]{3,2,1,0:T(8,128)(2,1)} %densities_ref.15, bf16[6,64,128,128]{3,2,1,0:T(8,128)(2,1)} %residuals_ref.17), custom_call_target="tpu_custom_call" | custom-call | tf_op jit(solution)/shard_map/pallas_call | solution.py:299
  33.9 2.2 %shard_map.62 = bf16[8,128,128]{2,1,0:T(8,128)(2,1)S(1)} custom-call(s32[65]{0:T(128)S(4)} %get-tuple-element.7.table_ref, f32[8,128]{1,0:T(8,128)S(1)} %get-tuple-element.8.coef_ref, bf16[6,64,128,128]{3,2,1,0:T(8,128)(2,1)} %densities_ref.15, bf16[6,64,128,128]{3,2,1,0:T(8,128)(2,1)} %residuals_ref.17), custom_call_target="tpu_custom_call" | custom-call | tf_op jit(solution)/shard_map/pallas_call | solution.py:299
  36.1 2.2 %shard_map.59 = bf16[8,128,128]{2,1,0:T(8,128)(2,1)S(1)} custom-call(s32[65]{0:T(128)S(4)} %get-tuple-element.7.table_ref, f32[8,128]{1,0:T(8,128)S(1)} %get-tuple-element.8.coef_ref, bf16[6,64,128,128]{3,2,1,0:T(8,128)(2,1)} %densities_ref.15, bf16[6,64,128,128]{3,2,1,0:T(8,128)(2,1)} %residuals_ref.17), custom_call_target="tpu_custom_call" | custom-call | tf_op jit(solution)/shard_map/pallas_call | solution.py:299
  38.2 6.0 %collective-permute-start = (bf16[8,128,128]{2,1,0:T(8,128)(2,1)S(1)}, bf16[8,128,128]{2,1,0:T(8,128)(2,1)S(1)}, u32[]{:S(2)}, u32[]{:S(2)}) collective-permute-start(bf16[8,128,128]{2,1,0:T(8,128)(2,1)S(1)} %shard_map.59), channel_id=1, source_target_pairs={{0,28},{4,24},{8,20},{12,16},{16,12},{20,8},{24,4},{28,0},{1,29},{... | collective-permute-start | bytes 786440 | tf_op jit(solution)/shard_map/ppermute | solution.py:399
  44.3 0.0 collective-permute-start.4
  44.3 1.1 %collective-permute-start.5 = (bf16[8,128,128]{2,1,0:T(8,128)(2,1)S(1)}, bf16[8,128,128]{2,1,0:T(8,128)(2,1)S(1)}, u32[]{:S(2)}, u32[]{:S(2)}) collective-permute-start(bf16[8,128,128]{2,1,0:T(8,128)(2,1)S(1)} %shard_map.63), channel_id=1, source_target_pairs={{0,4},{4,0},{8,12},{12,8},{16,20},{20,16},{24,28},{28,24},{1,5},{5... | collective-permute-start | bytes 786440 | tf_op jit(solution)/shard_map/ppermute | solution.py:399
  45.4 0.0 collective-permute-done.2.rest_1_
  45.4 0.3 collective-permute-start.6
  45.7 0.0 collective-permute-done.3.rest_2_
  45.7 3.5 %collective-permute-start.1 = (bf16[8,128,128]{2,1,0:T(8,128)(2,1)S(1)}, bf16[8,128,128]{2,1,0:T(8,128)(2,1)S(1)}, u32[]{:S(2)}, u32[]{:S(2)}) collective-permute-start(bf16[8,128,128]{2,1,0:T(8,128)(2,1)S(1)} %get-tuple-element.9), channel_id=1, source_target_pairs={{0,16},{4,20},{8,24},{12,28},{16,0},{20,4},{24,8},{28,12},{1,17},{... | collective-permute-start | bytes 786440 | tf_op jit(solution)/shard_map/ppermute | solution.py:399
  49.2 0.1 constant_dynamic-slice_fusion
  49.3 2.2 %shard_map.65.rest_6_ = bf16[8,128,128]{2,1,0:T(8,128)(2,1)S(1)} custom-call(s32[65]{0:T(128)S(4)} %get-tuple-element.7.table_ref, f32[8,128]{1,0:T(8,128)S(1)} %get-tuple-element.8.coef_ref, bf16[6,64,128,128]{3,2,1,0:T(8,128)(2,1)} %densities_ref.15, bf16[6,64,128,128]{3,2,1,0:T(8,128)(2,1)} %residuals_ref.17), custom_call_target="tpu_custom_call" | custom-call | tf_op jit(solution)/shard_map/pallas_call | solution.py:299
  51.5 0.1 copy.10
  51.6 0.2 select_reduce_fusion
  51.8 0.6 slice_reduce_fusion
  52.4 5.1 %collective-permute-done.4.rest_3_ = bf16[8,128,128]{2,1,0:T(8,128)(2,1)S(1)} collective-permute-done((bf16[8,128,128]{2,1,0:T(8,128)(2,1)S(1)}, bf16[8,128,128]{2,1,0:T(8,128)(2,1)S(1)}, u32[]{:S(2)}, u32[]{:S(2)}) %collective-permute-start.4) | collective-permute-done | bytes 262176 | tf_op jit(solution)/shard_map/ppermute | solution.py:399
  57.5 2.6 %collective-permute-done.5.rest_4_ = bf16[8,128,128]{2,1,0:T(8,128)(2,1)S(1)} collective-permute-done((bf16[8,128,128]{2,1,0:T(8,128)(2,1)S(1)}, bf16[8,128,128]{2,1,0:T(8,128)(2,1)S(1)}, u32[]{:S(2)}, u32[]{:S(2)}) %collective-permute-start.5) | collective-permute-done | bytes 262176 | tf_op jit(solution)/shard_map/ppermute | solution.py:399
  60.1 2.6 %collective-permute-done.6.rest_5_ = bf16[8,128,128]{2,1,0:T(8,128)(2,1)S(1)} collective-permute-done((bf16[8,128,128]{2,1,0:T(8,128)(2,1)S(1)}, bf16[8,128,128]{2,1,0:T(8,128)(2,1)S(1)}, u32[]{:S(2)}, u32[]{:S(2)}) %collective-permute-start.6) | collective-permute-done | bytes 262176 | tf_op jit(solution)/shard_map/ppermute | solution.py:399
  62.6 14.0 %collective-permute-done.1.rest_0_ = bf16[8,128,128]{2,1,0:T(8,128)(2,1)S(1)} collective-permute-done((bf16[8,128,128]{2,1,0:T(8,128)(2,1)S(1)}, bf16[8,128,128]{2,1,0:T(8,128)(2,1)S(1)}, u32[]{:S(2)}, u32[]{:S(2)}) %collective-permute-start.1) | collective-permute-done | bytes 262176 | tf_op jit(solution)/shard_map/ppermute | solution.py:399
  76.6 1.8 %place.2.rest_1_ = bf16[32,128,128]{2,1,0:T(8,128)(2,1)} custom-call(s32[8]{0:T(128)S(1)} %convert_element_type.6.count_ref, s32[8]{0:T(128)S(1)} %convert_element_type.7.offset_ref, bf16[8,128,128]{2,1,0:T(8,128)(2,1)S(1)} %collective-permute-done.1.rest_0_, bf16[8,128,128]{2,1,0:T(8,128)(2,1)S(1)} %collective-permute-done.2.rest_1_, ...), custom_call_target="tpu_custom_call" | custom-call | tf_op jit(solution)/shard_map/place/pallas_call | solution.py:349
  78.4 0.0 collective-permute-done.rest_0_
  78.4 0.6 place.3
  (3 shorter events, 0.0 us)
Async XLA Ops:
  8.6 14.4 %all-to-all-start = ((f32[32,1,128]{2,1,0:T(1,128)}), f32[32,1,128]{2,1,0:T(1,128)S(1)}, u32[]{:S(2)}, u32[]{:S(2)}) async-start(f32[32,1,128]{2,1,0:T(1,128)} %get-tuple-element.6), calls=%async_computation | async-start | bytes 32768 | tf_op jit(solution)/shard_map/all_to_all | solution.py:387
  25.6 19.8 %collective-permute-start.2 = (bf16[8,128,128]{2,1,0:T(8,128)(2,1)S(1)}, bf16[8,128,128]{2,1,0:T(8,128)(2,1)S(1)}, u32[]{:S(2)}, u32[]{:S(2)}) collective-permute-start(bf16[8,128,128]{2,1,0:T(8,128)(2,1)S(1)} %shard_map.60), channel_id=1, source_target_pairs={{0,20},{4,16},{8,28},{12,24},{16,4},{20,0},{24,12},{28,8},{1,21},{... | collective-permute-start | bytes 786440 | tf_op jit(solution)/shard_map/ppermute | solution.py:399
  28.4 17.3 %collective-permute-start.3 = (bf16[8,128,128]{2,1,0:T(8,128)(2,1)S(1)}, bf16[8,128,128]{2,1,0:T(8,128)(2,1)S(1)}, u32[]{:S(2)}, u32[]{:S(2)}) collective-permute-start(bf16[8,128,128]{2,1,0:T(8,128)(2,1)S(1)} %shard_map.61), channel_id=1, source_target_pairs={{0,8},{4,12},{8,0},{12,4},{16,24},{20,28},{24,16},{28,20},{1,9},{5... | collective-permute-start | bytes 786440 | tf_op jit(solution)/shard_map/ppermute | solution.py:399
  38.2 40.2 %collective-permute-start = (bf16[8,128,128]{2,1,0:T(8,128)(2,1)S(1)}, bf16[8,128,128]{2,1,0:T(8,128)(2,1)S(1)}, u32[]{:S(2)}, u32[]{:S(2)}) collective-permute-start(bf16[8,128,128]{2,1,0:T(8,128)(2,1)S(1)} %shard_map.59), channel_id=1, source_target_pairs={{0,28},{4,24},{8,20},{12,16},{16,12},{20,8},{24,4},{28,0},{1,29},{... | collective-permute-start | bytes 786440 | tf_op jit(solution)/shard_map/ppermute | solution.py:399
  44.3 13.2 %collective-permute-start.4 = (bf16[8,128,128]{2,1,0:T(8,128)(2,1)S(1)}, bf16[8,128,128]{2,1,0:T(8,128)(2,1)S(1)}, u32[]{:S(2)}, u32[]{:S(2)}) collective-permute-start(bf16[8,128,128]{2,1,0:T(8,128)(2,1)S(1)} %shard_map.62), channel_id=1, source_target_pairs={{0,12},{4,8},{8,4},{12,0},{16,28},{20,24},{24,20},{28,16},{1,13},{... | collective-permute-start | bytes 786440 | tf_op jit(solution)/shard_map/ppermute | solution.py:399
  44.3 15.8 %collective-permute-start.5 = (bf16[8,128,128]{2,1,0:T(8,128)(2,1)S(1)}, bf16[8,128,128]{2,1,0:T(8,128)(2,1)S(1)}, u32[]{:S(2)}, u32[]{:S(2)}) collective-permute-start(bf16[8,128,128]{2,1,0:T(8,128)(2,1)S(1)} %shard_map.63), channel_id=1, source_target_pairs={{0,4},{4,0},{8,12},{12,8},{16,20},{20,16},{24,28},{28,24},{1,5},{5... | collective-permute-start | bytes 786440 | tf_op jit(solution)/shard_map/ppermute | solution.py:399
  45.4 17.2 %collective-permute-start.6 = (bf16[8,128,128]{2,1,0:T(8,128)(2,1)S(1)}, bf16[8,128,128]{2,1,0:T(8,128)(2,1)S(1)}, u32[]{:S(2)}, u32[]{:S(2)}) collective-permute-start(bf16[8,128,128]{2,1,0:T(8,128)(2,1)S(1)} %shard_map.64), channel_id=1, source_target_pairs={{0,24},{4,28},{8,16},{12,20},{16,8},{20,12},{24,0},{28,4},{1,25},{... | collective-permute-start | bytes 786440 | tf_op jit(solution)/shard_map/ppermute | solution.py:399
  45.7 30.9 %collective-permute-start.1 = (bf16[8,128,128]{2,1,0:T(8,128)(2,1)S(1)}, bf16[8,128,128]{2,1,0:T(8,128)(2,1)S(1)}, u32[]{:S(2)}, u32[]{:S(2)}) collective-permute-start(bf16[8,128,128]{2,1,0:T(8,128)(2,1)S(1)} %get-tuple-element.9), channel_id=1, source_target_pairs={{0,16},{4,20},{8,24},{12,28},{16,0},{20,4},{24,8},{28,12},{1,17},{... | collective-permute-start | bytes 786440 | tf_op jit(solution)/shard_map/ppermute | solution.py:399
